TPU v7x, 32 devices: a whole 2x2x4 slice. The times are simulated.
32 devices in a mesh: wide: 8 (over z, x), narrow: 4 (over y, core).
Axes of the slice: x: 2, y: 2, z: 4, core: 2. Of those that a mesh axis runs over, the one named last changes fastest.
Arguments:
- activations: bfloat16 [2048, 16384], P('wide', 'narrow'), may hold values from -6 to 6
- grad_out: bfloat16 [2048, 8192], P('narrow', 'wide'), may hold values from -0.125 to 0.125
- momentum: float32 [8192, 16384], P('wide', 'narrow'), may hold values from -90 to 90
- right_factor: float32 [16384, 512], P('narrow'), may hold values from -0.046875 to 0.046875
Outputs:
- new_momentum: float32 [8192, 16384], P('wide', 'narrow')
- new_right: float32 [16384, 512], P('narrow')
- update: bfloat16 [8192, 16384], P('wide', 'narrow')
All inputs are finite; a program needn't handle non-finite values.
Results may differ from a plain program's by a relative error of at most 0.0012.
Values may be sent and summed in bfloat16 or wider, within the bound.
No kernel may reach another device: no remote copies, remote signals or barrier semaphores. Data moves between devices by JAX's collectives and lax.ppermute only.
A program may use at most 128 MiB of HBM per device.

v0:
```python
import math
import jax
import jax.numpy as jnp
from jax import lax
from jax.sharding import PartitionSpec as P

DOUT = 8192
DIN = 16384
RANK = 512
FEEDBACK = 0.05
EPSILON = 1e-06


def body(activations, grad_out, momentum, right_factor):
    highest = lax.Precision.HIGHEST
    out_rows = lax.all_gather(grad_out, "narrow", axis=0, tiled=True)
    gradient = lax.dot_general(
        out_rows,
        lax.all_gather(activations, "wide", axis=0, tiled=True),
        (((0,), (0,)), ((), ())),
        preferred_element_type=jnp.float32,
    )
    buffer = momentum + gradient
    partial_left = jnp.dot(
        buffer, right_factor, precision=highest, preferred_element_type=jnp.float32
    )
    left_factor = lax.psum(partial_left, "narrow")
    gram_local = jnp.dot(
        left_factor.T, left_factor, precision=highest, preferred_element_type=jnp.float32
    )
    gram_matrix = lax.psum(gram_local, "wide")
    lower_factor = jnp.linalg.cholesky(gram_matrix)
    ortho_left = jax.scipy.linalg.solve_triangular(lower_factor, left_factor.T, lower=True).T
    right_share = lax.psum_scatter(
        lax.dot_general(
            buffer,
            ortho_left,
            (((0,), (0,)), ((), ())),
            precision=highest,
            preferred_element_type=jnp.float32,
        ),
        "wide",
        scatter_dimension=0,
        tiled=True,
    )
    col_squares = lax.psum(jnp.sum(right_share * right_share, axis=0), ("wide", "narrow"))
    right_raw = lax.all_gather(right_share, "wide", axis=0, tiled=True)
    feedback = lax.dot_general(
        ortho_left,
        right_raw,
        (((1,), (1,)), ((), ())),
        precision=highest,
        preferred_element_type=jnp.float32,
    )
    new_momentum = buffer - FEEDBACK * feedback
    new_right = right_raw / (jnp.sqrt(col_squares) + EPSILON)
    update_scale = math.sqrt(DOUT * DIN / RANK)
    product = lax.dot_general(
        ortho_left,
        new_right,
        (((1,), (1,)), ((), ())),
        precision=highest,
        preferred_element_type=jnp.float32,
    )
    update = (update_scale * product).astype(jnp.bfloat16)
    return (new_momentum, new_right, update)


def solution(mesh):
    return jax.shard_map(
        body,
        mesh=mesh,
        in_specs=(P("wide", "narrow"), P("narrow", "wide"), P("wide", "narrow"), P("narrow", None)),
        out_specs=(P("wide", "narrow"), P("narrow", None), P("wide", "narrow")),
        check_vma=False,
    )
```

profile of v0, /device:TPU:0, one launch (start us, length us, event | category | flops | bytes accessed | tf_op | source)
XLA Modules:
  0.0 1089.3 jit_solution(18141778755275494876)
XLA Ops:
  7.2 0.7 all-gather.4.cloned.1.call-update
  7.9 0.7 all-gather.6.cloned.1.call-update
  8.6 0.0 all-reduce.4.cloned.1.call-start
  8.7 38.1 %all-gather.4.cloned.1.call-done = bf16[2048,1024]{1,0:T(8,128)(2,1)} async-done(((bf16[512,1024]{1,0:T(8,128)(2,1)}), bf16[2048,1024]{1,0:T(8,128)(2,1)}) %all-gather.4.cloned.1.call-update) | async-done | bytes 4194320 | tf_op jit(solution)/shard_map/all_gather | solution.py:16
  46.7 229.4 %all-gather.6.cloned.1.call-done = bf16[2048,4096]{1,0:T(8,128)(2,1)} async-done(((bf16[256,4096]{1,0:T(8,128)(2,1)}), bf16[2048,4096]{1,0:T(8,128)(2,1)}) %all-gather.6.cloned.1.call-update) | async-done | bytes 16777232 | tf_op jit(solution)/shard_map/all_gather | solution.py:19
  276.2 28.3 %convolution_add_fusion = f32[1024,4096]{1,0:T(8,128)} fusion(f32[1024,4096]{1,0:T(8,128)} %param.6, bf16[2048,1024]{1,0:T(8,128)(2,1)} %all-gather.4.cloned.1.call-done, bf16[2048,4096]{1,0:T(8,128)(2,1)} %all-gather.6.cloned.1.call-done), kind=kOutput, calls=%fused_computation.4 | convolution fusion | flops 17184063488 | bytes 54525952 | tf_op jit(solution)/shard_map/dot_general | solution.py:17
  304.5 31.4 %fusion.39 = f32[1024,512]{1,0:T(8,128)} fusion(f32[1024,4096]{1,0:T(8,128)} %convolution_add_fusion, f32[4096,512]{1,0:T(8,128)} %param.7), kind=kOutput, calls=%fused_computation.78 | convolution fusion | flops 25769803776 | bytes 27262976 | tf_op jit(solution)/shard_map/dot_general | solution.py:24
  335.9 0.0 all-reduce.6.cloned.1.call-start
  336.0 49.7 %all-reduce.4.cloned.1.call-done = f32[1024,512]{1,0:T(8,128)} async-done(((f32[1024,512]{1,0:T(8,128)}), f32[1024,512]{1,0:T(8,128)}) %all-reduce.4.cloned.1.call-update) | async-done | bytes 2097168 | tf_op jit(solution)/shard_map/psum | solution.py:27
  385.6 6.7 fusion.40
  392.4 0.2 reduce-scatter.2.cloned.1.call-start
  392.6 78.3 %all-reduce.6.cloned.1.call-done = f32[512,512]{0,1:T(8,128)} async-done(((f32[512,512]{0,1:T(8,128)}), f32[512,512]{0,1:T(8,128)}) %all-reduce.6.cloned.1.call-update) | async-done | bytes 1048592 | tf_op jit(solution)/shard_map/psum | solution.py:31
  470.9 1.6 copy.8
  472.5 1.4 fusion.12
  473.9 1.0 copy-done.3
  474.9 11.7 %cholesky.104 = f32[128,128]{1,0:T(8,128)S(1)} custom-call(f32[128,128]{1,0:T(8,128)S(1)} %cholesky.266), custom_call_target="Cholesky" | custom-call | tf_op jit(solution)/shard_map/jit(cholesky)/cholesky | solution.py:32
  486.7 0.1 cholesky.224
  486.8 9.8 custom-call.31
  496.6 1.2 constant_dynamic-update-slice_fusion.3
  497.8 1.3 convolution_subtract_fusion.2
  499.1 11.7 %cholesky.217 = f32[128,128]{1,0:T(8,128)S(1)} custom-call(f32[128,128]{1,0:T(8,128)S(1)} %cholesky.270), custom_call_target="Cholesky" | custom-call | tf_op jit(solution)/shard_map/jit(cholesky)/cholesky | solution.py:32
  510.9 10.0 custom-call.32
  520.9 0.3 convolution_dynamic-update-slice_fusion
  521.1 1.3 convolution_subtract_fusion.3
  522.5 11.7 %cholesky.238 = f32[128,128]{1,0:T(8,128)S(1)} custom-call(f32[128,128]{1,0:T(8,128)S(1)} %cholesky.275), custom_call_target="Cholesky" | custom-call | tf_op jit(solution)/shard_map/jit(cholesky)/cholesky | solution.py:32
  534.2 9.8 custom-call.33
  544.0 0.2 convolution_dynamic-update-slice_fusion.1
  544.2 1.2 convolution_subtract_fusion.4
  545.5 11.7 %cholesky.255 = f32[128,128]{1,0:T(8,128)S(1)} custom-call(f32[128,128]{1,0:T(8,128)S(1)} %convolution_subtract_fusion.4), custom_call_target="Cholesky" | custom-call | tf_op jit(solution)/shard_map/jit(cholesky)/cholesky | solution.py:32
  557.2 0.7 compare_reduce_fusion.1
  557.9 0.6 compare_reduce_fusion
  558.5 0.7 compare_reduce_fusion.2
  561.7 1.6 select_select_fusion
  563.3 13.6 %while.1 = (s32[]{:T(128)}, f32[512,512]{1,0:T(8,128)}, s32[4,2]{0,1:T(2,128)S(1)}, f32[4,128,128]{2,1,0:T(8,128)}, s32[]{:T(128)}) while((s32[]{:T(128)}, f32[512,512]{1,0:T(8,128)}, s32[4,2]{0,1:T(2,128)S(1)}, f32[4,128,128]{2,1,0:T(8,128)}, s32[]{:T(128)}) %tuple.31), condition=%wide.while_cond, body=%wide.while_body.sunk | while | flops 2 | bytes 132205 | solution.py:33
  563.3 0.1 constant_dynamic-slice_fusion.2
  563.3 0.5 fusion.56
  563.9 2.8 bitcast_dynamic-update-slice_fusion.2
  566.7 0.1 constant_dynamic-slice_fusion.2
  566.8 0.5 fusion.56
  567.3 2.8 bitcast_dynamic-update-slice_fusion.2
  570.1 0.1 constant_dynamic-slice_fusion.2
  570.2 0.5 fusion.56
  570.7 2.8 bitcast_dynamic-update-slice_fusion.2
  573.5 0.1 constant_dynamic-slice_fusion.2
  573.6 0.5 fusion.56
  574.1 2.8 bitcast_dynamic-update-slice_fusion.2
  576.9 40.1 %custom-call.34 = f32[4,128,128]{1,2,0:T(8,128)S(1)} custom-call(f32[4,128,128]{2,1,0:T(8,128)} %get-tuple-element.10), custom_call_target="InvertDiagBlocksLowerTriangular" | custom-call | tf_op jit(solution)/shard_map/jit(_solve_triangular)/triangular_solve | solution.py:33
  617.0 0.6 fusion.13
  617.7 1.8 convolution_subtract_fusion.1
  619.5 0.6 fusion.27
  620.2 2.9 convolution_subtract_fusion
  623.0 0.6 fusion.25
  623.7 3.8 fusion.6
  627.5 0.6 fusion.24
  628.2 0.8 copy-done.4
  629.0 56.3 %fusion.15 = f32[4096,512]{1,0:T(8,128)} fusion(f32[1024,4096]{1,0:T(8,128)} %convolution_add_fusion, f32[128,1024]{1,0:T(8,128)S(1)} %fusion.24, f32[128,1024]{1,0:T(8,128)S(1)} %fusion.25, f32[128,1024]{1,0:T(8,128)S(1)} %fusion.27, f32[128,1024]{1,0:T(8,128)S(1)} %fusion.13), kind=kOutput, calls=%fused_computation.31 | convolution fusion | flops 25771376640 | bytes 27262976 | tf_op jit(solution)/shard_map/dot_general | solution.py:35
  685.3 0.0 all-gather.8.cloned.1.call-start
  685.4 147.2 %reduce-scatter.2.cloned.1.call-done = f32[512,512]{1,0:T(8,128)} async-done(((f32[4096,512]{1,0:T(8,128)}), f32[512,512]{1,0:T(8,128)}) %reduce-scatter.2.cloned.1.call-update) | async-done | bytes 1048592 | tf_op jit(solution)/shard_map/reduce_scatter | solution.py:34
  832.6 1.3 multiply_reduce_fusion
  833.9 43.3 %psum.23 = f32[512]{0:T(512)S(1)} all-reduce(f32[512]{0:T(512)S(1)} %multiply_reduce_fusion), channel_id=1, replica_groups=mesh['wide'=8,'narrow'=4] {'wide','narrow'}, use_global_device_ids=true, to_apply=%region_12.13 | all-reduce | flops 512 | bytes 4096 | tf_op jit(solution)/shard_map/psum | solution.py:46
  877.2 82.0 %all-gather.8.cloned.1.call-done = f32[4096,512]{1,0:T(8,128)} async-done(((f32[512,512]{1,0:T(8,128)}), f32[4096,512]{1,0:T(8,128)}) %all-gather.8.cloned.1.call-update) | async-done | bytes 8388624 | tf_op jit(solution)/shard_map/all_gather | solution.py:47
  959.2 8.9 broadcast_divide_fusion
  968.1 56.8 %multiply_convert_fusion = bf16[1024,4096]{1,0:T(8,128)(2,1)} fusion(f32[4096,512]{1,0:T(8,128)} %broadcast_divide_fusion, f32[128,1024]{1,0:T(8,128)} %copy-done.4, f32[128,1024]{1,0:T(8,128)} %copy-done.2, f32[128,1024]{1,0:T(8,128)} %copy-done.1, f32[128,1024]{1,0:T(8,128)S(1)} %fusion.13), kind=kOutput, calls=%fused_computation.2 | convolution fusion | flops 25779765248 | bytes 18874368 | tf_op jit(solution)/shard_map/dot_general | solution.py:58
  1025.0 57.3 %multiply_subtract_fusion = f32[1024,4096]{1,0:T(8,128)} fusion(f32[1024,4096]{1,0:T(8,128)S(1)} %bitcast.65, f32[4096,512]{1,0:T(8,128)S(1)} %bitcast.59, f32[128,1024]{1,0:T(8,128)} %copy-done.4, f32[128,1024]{1,0:T(8,128)} %copy-done.2, f32[128,1024]{1,0:T(8,128)} %copy-done.1, f32[128,1024]{1,0:T(8,128)S(1)} %fusion.13), kind=kOutput, calls=%fused_computation.3 | convolution fusion | flops 25779765248 | bytes 44040192 | tf_op jit(solution)/shard_map/dot_general | solution.py:48
  (39 shorter events, 0.4 us)
Async XLA Ops:
  7.2 39.6 %all-gather.4.cloned.1.call-start = ((), (), s32[]{:S(2)}) async-start(), calls=%async_computation.1 | async-start | bytes 5242880 | tf_op jit(solution)/shard_map/all_gather | solution.py:16
  7.9 268.3 %all-gather.6.cloned.1.call-start = ((), (), s32[]{:S(2)}) async-start(), calls=%async_computation.2 | async-start | bytes 18874368 | tf_op jit(solution)/shard_map/all_gather | solution.py:19
  8.6 377.0 %all-reduce.4.cloned.1.call-start = ((), (), s32[]{:S(2)}) async-start(), calls=%async_computation.3 | async-start | bytes 4194304 | tf_op jit(solution)/shard_map/psum | solution.py:27
  335.9 135.0 %all-reduce.6.cloned.1.call-start = ((), (), s32[]{:S(2)}) async-start(), calls=%async_computation.4 | async-start | bytes 2097152 | tf_op jit(solution)/shard_map/psum | solution.py:31
  392.4 440.2 %reduce-scatter.2.cloned.1.call-start = ((), (), s32[]{:S(2)}) async-start(), calls=%async_computation.5 | async-start | bytes 9437184 | tf_op jit(solution)/shard_map/reduce_scatter | solution.py:34
  473.9 1.0 copy-start.3
  474.9 142.1 %copy-start = (f32[1024,512]{1,0:T(8,128)S(1)}, f32[1024,512]{1,0:T(8,128)}, u32[]{:S(2)}) copy-start(f32[1024,512]{1,0:T(8,128)} %all-reduce.4.cloned.1.call-done) | copy-start | bytes 6291460
  620.2 65.1 %copy-start.1 = (f32[128,1024]{1,0:T(8,128)}, f32[128,1024]{1,0:T(8,128)S(1)}, u32[]{:S(2)}) copy-start(f32[128,1024]{1,0:T(8,128)S(1)} %fusion.27) | copy-start | bytes 1572868
  623.7 4.5 copy-start.2
  628.2 0.8 copy-start.4
  685.3 273.9 %all-gather.8.cloned.1.call-start = ((), (), s32[]{:S(2)}) async-start(), calls=%async_computation.6 | async-start | bytes 9437184 | tf_op jit(solution)/shard_map/all_gather | solution.py:47
  959.2 65.7 %slice-start = ((s8[8388608]{0:T(1024)(128)(4,1)}), s8[4194304]{0:T(1024)(128)(4,1)S(1)}, s32[]{:S(2)}) async-start(s8[8388608]{0:T(1024)(128)(4,1)} %bitcast.58), calls=%async_computation.7 | async-start | bytes 8388608
  959.2 65.7 %slice-start.2 = ((s8[16777216]{0:T(1024)(128)(4,1)}), s8[4194304]{0:T(1024)(128)(4,1)S(1)}, s32[]{:S(2)}) async-start(s8[16777216]{0:T(1024)(128)(4,1)} %bitcast.64), calls=%async_computation.9 | async-start | bytes 8388608
  959.2 65.7 %slice-start.3 = ((s8[16777216]{0:T(1024)(128)(4,1)}), s8[4194304]{0:T(1024)(128)(4,1)S(1)}, s32[]{:S(2)}) async-start(s8[16777216]{0:T(1024)(128)(4,1)} %bitcast.64), calls=%async_computation.10 | async-start | bytes 8388608
  968.1 56.8 %slice-start.1 = ((s8[8388608]{0:T(1024)(128)(4,1)}), s8[4194304]{0:T(1024)(128)(4,1)S(1)}, s32[]{:S(2)}) async-start(s8[8388608]{0:T(1024)(128)(4,1)} %bitcast.58), calls=%async_computation.8 | async-start | bytes 8388608
  968.1 56.8 %slice-start.4 = ((s8[16777216]{0:T(1024)(128)(4,1)}), s8[4194304]{0:T(1024)(128)(4,1)S(1)}, s32[]{:S(2)}) async-start(s8[16777216]{0:T(1024)(128)(4,1)} %bitcast.64), calls=%async_computation.11 | async-start | bytes 8388608
  968.1 56.8 %slice-start.5 = ((s8[16777216]{0:T(1024)(128)(4,1)}), s8[4194304]{0:T(1024)(128)(4,1)S(1)}, s32[]{:S(2)}) async-start(s8[16777216]{0:T(1024)(128)(4,1)} %bitcast.64), calls=%async_computation.12 | async-start | bytes 8388608
Sparse Core Ops, SparseCore 0:
  9.5 37.1 all-gather.3
  48.9 227.2 all-gather.5
  336.0 49.5 all-reduce.3
  392.5 78.3 all-reduce.5
  685.4 147.0 reduce-scatter.1
  834.5 124.6 all-gather.7
where the time goes:
time: 1100 us; the launch traced here: 1090 us
  waiting for transfers between devices  626 us (57%)
  matrix products  253 us (23%)
  other arithmetic  132 us (12%)
  blocking collectives  43.3 us (4%)
  local copies, waits for them, and re-layouts  17.1 us (2%)
  between operations  17.1 us (2%)
    all_gather x1, waiting for transfers between devices, body(): lax.all_gather(activations, 'wide', axis=0, tiled=True)  229 us
    reduce_scatter x1, waiting for transfers between devices, body(): lax.psum_scatter(lax.dot_general(buffer, ortho_left, (((0,), (0,)), ((),...  147 us
    all_gather x1, waiting for transfers between devices, body(): right_raw = lax.all_gather(right_share, 'wide', axis=0, tiled=True)  82 us
    another operation x14, other arithmetic, body(): lower_factor = jnp.linalg.cholesky(gram_matrix)  78.6 us
    psum x1, waiting for transfers between devices, body(): gram_matrix = lax.psum(gram_local, 'wide')  78.3 us
    dot_general x1, matrix products, body(): lax.dot_general(ortho_left, right_raw, (((1,), (1,)), ((), ())), precisio...  57.3 us
    dot_general x1, matrix products, body(): lax.dot_general(ortho_left, new_right, (((1,), (1,)), ((), ())), precisio...  56.8 us
    dot_general x1, matrix products, body(): lax.dot_general(buffer, ortho_left, (((0,), (0,)), ((), ())), precision=h...  56.3 us
  transfers between devices with their start and end apart: 6, of which 6 were waited for; matrix products, arithmetic and copies ran while one was open for 0% of the time, Pallas kernels for 0%

commit v1 on v0

--- a/solution.py
+++ b/solution.py
@@ -28,7 +28,7 @@
     gram_local = jnp.dot(
         left_factor.T, left_factor, precision=highest, preferred_element_type=jnp.float32
     )
-    gram_matrix = lax.psum(gram_local, "wide")
+    gram_matrix = jnp.sum(lax.all_gather(gram_local, "wide"), axis=0)
     lower_factor = jnp.linalg.cholesky(gram_matrix)
     ortho_left = jax.scipy.linalg.solve_triangular(lower_factor, left_factor.T, lower=True).T
     right_share = lax.psum_scatter(

time: 1100 us -> 1140 us (1.036)
  waiting for transfers between devices: 626 us -> 671 us
    all_gather x0 -> x1, waiting for transfers between devices: none -> 124 us  [body(): gram_matrix = jnp.sum(lax.all_gather(gram_local, 'wide'), axis=0)]
    psum x1 -> x0, waiting for transfers between devices: 78.3 us -> none  [body(): gram_matrix = lax.psum(gram_local, 'wide')]
where the time goes in v1:
time: 1140 us
  waiting for transfers between devices  671 us (59%)
  matrix products  253 us (22%)
  other arithmetic  135 us (12%)
  blocking collectives  43.3 us (4%)
  between operations  17.1 us (2%)
  local copies, waits for them, and re-layouts  15.8 us (1%)
    all_gather x1, waiting for transfers between devices, body(): lax.all_gather(activations, 'wide', axis=0, tiled=True)  229 us
    reduce_scatter x1, waiting for transfers between devices, body(): lax.psum_scatter(lax.dot_general(buffer, ortho_left, (((0,), (0,)), ((),...  146 us
    all_gather x1, waiting for transfers between devices, body(): gram_matrix = jnp.sum(lax.all_gather(gram_local, 'wide'), axis=0)  124 us
    all_gather x1, waiting for transfers between devices, body(): right_raw = lax.all_gather(right_share, 'wide', axis=0, tiled=True)  82 us
    another operation x14, other arithmetic, body(): lower_factor = jnp.linalg.cholesky(gram_matrix)  79.1 us
    dot_general x1, matrix products, body(): lax.dot_general(ortho_left, right_raw, (((1,), (1,)), ((), ())), precisio...  57.3 us
    dot_general x1, matrix products, body(): lax.dot_general(ortho_left, new_right, (((1,), (1,)), ((), ())), precisio...  56.8 us
    dot_general x1, matrix products, body(): lax.dot_general(buffer, ortho_left, (((0,), (0,)), ((), ())), precision=h...  56.3 us
  transfers between devices with their start and end apart: 6, of which 6 were waited for; matrix products, arithmetic and copies ran while one was open for 0% of the time, Pallas kernels for 0%

profile of v1, /device:TPU:0, one launch (start us, length us, event | category | flops | bytes accessed | tf_op | source)
XLA Modules:
  0.0 1136.0 jit_solution(14320133369232768248)
XLA Ops:
  7.2 0.7 all-gather.6.cloned.1.call-update
  7.9 0.7 all-gather.8.cloned.1.call-update
  8.7 38.1 %all-gather.6.cloned.1.call-done = bf16[2048,1024]{1,0:T(8,128)(2,1)} async-done(((bf16[512,1024]{1,0:T(8,128)(2,1)}), bf16[2048,1024]{1,0:T(8,128)(2,1)}) %all-gather.6.cloned.1.call-update) | async-done | bytes 4194320 | tf_op jit(solution)/shard_map/all_gather | solution.py:16
  46.7 229.4 %all-gather.8.cloned.1.call-done = bf16[2048,4096]{1,0:T(8,128)(2,1)} async-done(((bf16[256,4096]{1,0:T(8,128)(2,1)}), bf16[2048,4096]{1,0:T(8,128)(2,1)}) %all-gather.8.cloned.1.call-update) | async-done | bytes 16777232 | tf_op jit(solution)/shard_map/all_gather | solution.py:19
  276.2 28.3 %convolution_add_fusion = f32[1024,4096]{1,0:T(8,128)} fusion(f32[1024,4096]{1,0:T(8,128)} %param.6, bf16[2048,1024]{1,0:T(8,128)(2,1)} %all-gather.6.cloned.1.call-done, bf16[2048,4096]{1,0:T(8,128)(2,1)} %all-gather.8.cloned.1.call-done), kind=kOutput, calls=%fused_computation.4 | convolution fusion | flops 17184063488 | bytes 54525952 | tf_op jit(solution)/shard_map/dot_general | solution.py:17
  304.5 31.4 %fusion.39 = f32[1024,512]{1,0:T(8,128)} fusion(f32[1024,4096]{1,0:T(8,128)} %convolution_add_fusion, f32[4096,512]{1,0:T(8,128)} %param.7), kind=kOutput, calls=%fused_computation.78 | convolution fusion | flops 25769803776 | bytes 27262976 | tf_op jit(solution)/shard_map/dot_general | solution.py:24
  335.9 0.0 all-gather.12.cloned.1.call-start
  336.0 49.7 %all-reduce.3.cloned.1.call-done = f32[1024,512]{1,0:T(8,128)} async-done(((f32[1024,512]{1,0:T(8,128)}), f32[1024,512]{1,0:T(8,128)}) %all-reduce.3.cloned.1.call-update) | async-done | bytes 2097168 | tf_op jit(solution)/shard_map/psum | solution.py:27
  385.6 6.7 fusion.40
  392.3 0.2 reduce-scatter.2.cloned.1.call-start
  392.6 124.4 %all-gather.12.cloned.1.call-done = f32[4096,512]{1,0:T(8,128)} async-done(((f32[512,512]{1,0:T(8,128)}), f32[4096,512]{1,0:T(8,128)}) %all-gather.12.cloned.1.call-update) | async-done | bytes 8388624 | tf_op jit(solution)/shard_map/all_gather | solution.py:31
  517.0 4.5 reduce_sum.18
  521.5 0.3 copy.8
  521.8 0.2 fusion.12
  522.1 1.0 copy-done.3
  523.1 11.7 %cholesky.104 = f32[128,128]{1,0:T(8,128)S(1)} custom-call(f32[128,128]{1,0:T(8,128)S(1)} %cholesky.266), custom_call_target="Cholesky" | custom-call | tf_op jit(solution)/shard_map/jit(cholesky)/cholesky | solution.py:32
  534.8 0.1 cholesky.224
  534.9 9.8 custom-call.31
  544.8 1.2 constant_dynamic-update-slice_fusion.3
  546.0 1.3 convolution_subtract_fusion.2
  547.3 11.9 %cholesky.217 = f32[128,128]{1,0:T(8,128)S(1)} custom-call(f32[128,128]{1,0:T(8,128)S(1)} %cholesky.270), custom_call_target="Cholesky" | custom-call | tf_op jit(solution)/shard_map/jit(cholesky)/cholesky | solution.py:32
  559.2 9.8 custom-call.32
  569.0 0.3 convolution_dynamic-update-slice_fusion
  569.3 1.3 convolution_subtract_fusion.3
  570.6 11.7 %cholesky.238 = f32[128,128]{1,0:T(8,128)S(1)} custom-call(f32[128,128]{1,0:T(8,128)S(1)} %cholesky.275), custom_call_target="Cholesky" | custom-call | tf_op jit(solution)/shard_map/jit(cholesky)/cholesky | solution.py:32
  582.4 9.8 custom-call.33
  592.2 0.2 convolution_dynamic-update-slice_fusion.1
  592.4 1.2 convolution_subtract_fusion.4
  593.6 12.2 %cholesky.255 = f32[128,128]{1,0:T(8,128)S(1)} custom-call(f32[128,128]{1,0:T(8,128)S(1)} %convolution_subtract_fusion.4), custom_call_target="Cholesky" | custom-call | tf_op jit(solution)/shard_map/jit(cholesky)/cholesky | solution.py:32
  605.8 0.6 compare_reduce_fusion.1
  606.5 0.6 compare_reduce_fusion
  607.1 0.7 compare_reduce_fusion.2
  610.3 1.1 select_select_fusion
  611.4 13.6 %while.1 = (s32[]{:T(128)}, f32[512,512]{1,0:T(8,128)}, s32[4,2]{0,1:T(2,128)S(1)}, f32[4,128,128]{2,1,0:T(8,128)}, s32[]{:T(128)}) while((s32[]{:T(128)}, f32[512,512]{1,0:T(8,128)}, s32[4,2]{0,1:T(2,128)S(1)}, f32[4,128,128]{2,1,0:T(8,128)}, s32[]{:T(128)}) %tuple.31), condition=%wide.while_cond, body=%wide.while_body.sunk | while | flops 2 | bytes 132205 | solution.py:33
  611.4 0.1 constant_dynamic-slice_fusion.2
  611.5 0.5 fusion.56
  612.0 2.8 bitcast_dynamic-update-slice_fusion.2
  614.9 0.1 constant_dynamic-slice_fusion.2
  614.9 0.5 fusion.56
  615.5 2.8 bitcast_dynamic-update-slice_fusion.2
  618.3 0.1 constant_dynamic-slice_fusion.2
  618.3 0.5 fusion.56
  618.9 2.8 bitcast_dynamic-update-slice_fusion.2
  621.7 0.1 constant_dynamic-slice_fusion.2
  621.7 0.5 fusion.56
  622.3 2.7 bitcast_dynamic-update-slice_fusion.2
  625.0 40.1 %custom-call.34 = f32[4,128,128]{1,2,0:T(8,128)S(1)} custom-call(f32[4,128,128]{2,1,0:T(8,128)} %get-tuple-element.10), custom_call_target="InvertDiagBlocksLowerTriangular" | custom-call | tf_op jit(solution)/shard_map/jit(_solve_triangular)/triangular_solve | solution.py:33
  665.2 0.6 fusion.13
  665.8 1.8 convolution_subtract_fusion.1
  667.7 0.6 fusion.27
  668.3 2.9 convolution_subtract_fusion
  671.2 0.6 fusion.25
  671.8 3.8 fusion.6
  675.7 0.6 fusion.24
  676.3 0.8 copy-done.4
  677.1 56.3 %fusion.15 = f32[4096,512]{1,0:T(8,128)} fusion(f32[1024,4096]{1,0:T(8,128)} %convolution_add_fusion, f32[128,1024]{1,0:T(8,128)S(1)} %fusion.24, f32[128,1024]{1,0:T(8,128)S(1)} %fusion.25, f32[128,1024]{1,0:T(8,128)S(1)} %fusion.27, f32[128,1024]{1,0:T(8,128)S(1)} %fusion.13), kind=kOutput, calls=%fused_computation.31 | convolution fusion | flops 25771376640 | bytes 27262976 | tf_op jit(solution)/shard_map/dot_general | solution.py:35
  733.4 0.0 all-gather.10.cloned.1.call-start
  733.5 145.7 %reduce-scatter.2.cloned.1.call-done = f32[512,512]{1,0:T(8,128)} async-done(((f32[4096,512]{1,0:T(8,128)}), f32[512,512]{1,0:T(8,128)}) %reduce-scatter.2.cloned.1.call-update) | async-done | bytes 1048592 | tf_op jit(solution)/shard_map/reduce_scatter | solution.py:34
  879.3 1.3 multiply_reduce_fusion
  880.6 43.3 %psum.15 = f32[512]{0:T(512)S(1)} all-reduce(f32[512]{0:T(512)S(1)} %multiply_reduce_fusion), channel_id=1, replica_groups=mesh['wide'=8,'narrow'=4] {'wide','narrow'}, use_global_device_ids=true, to_apply=%region_12.13 | all-reduce | flops 512 | bytes 4096 | tf_op jit(solution)/shard_map/psum | solution.py:46
  923.9 82.0 %all-gather.10.cloned.1.call-done = f32[4096,512]{1,0:T(8,128)} async-done(((f32[512,512]{1,0:T(8,128)}), f32[4096,512]{1,0:T(8,128)}) %all-gather.10.cloned.1.call-update) | async-done | bytes 8388624 | tf_op jit(solution)/shard_map/all_gather | solution.py:47
  1005.9 8.9 broadcast_divide_fusion
  1014.8 56.8 %multiply_convert_fusion = bf16[1024,4096]{1,0:T(8,128)(2,1)} fusion(f32[4096,512]{1,0:T(8,128)} %broadcast_divide_fusion, f32[128,1024]{1,0:T(8,128)} %copy-done.4, f32[128,1024]{1,0:T(8,128)} %copy-done.2, f32[128,1024]{1,0:T(8,128)} %copy-done.1, f32[128,1024]{1,0:T(8,128)S(1)} %fusion.13), kind=kOutput, calls=%fused_computation.2 | convolution fusion | flops 25779765248 | bytes 18874368 | tf_op jit(solution)/shard_map/dot_general | solution.py:58
  1071.7 57.3 %multiply_subtract_fusion = f32[1024,4096]{1,0:T(8,128)} fusion(f32[1024,4096]{1,0:T(8,128)S(1)} %bitcast.66, f32[4096,512]{1,0:T(8,128)S(1)} %bitcast.60, f32[128,1024]{1,0:T(8,128)} %copy-done.4, f32[128,1024]{1,0:T(8,128)} %copy-done.2, f32[128,1024]{1,0:T(8,128)} %copy-done.1, f32[128,1024]{1,0:T(8,128)S(1)} %fusion.13), kind=kOutput, calls=%fused_computation.3 | convolution fusion | flops 25779765248 | bytes 44040192 | tf_op jit(solution)/shard_map/dot_general | solution.py:48
  (40 shorter events, 0.4 us)
Async XLA Ops:
  7.2 39.6 %all-gather.6.cloned.1.call-start = ((), (), s32[]{:S(2)}) async-start(), calls=%async_computation.1 | async-start | bytes 5242880 | tf_op jit(solution)/shard_map/all_gather | solution.py:16
  7.9 268.3 %all-gather.8.cloned.1.call-start = ((), (), s32[]{:S(2)}) async-start(), calls=%async_computation.2 | async-start | bytes 18874368 | tf_op jit(solution)/shard_map/all_gather | solution.py:19
  8.6 377.0 %all-reduce.3.cloned.1.call-start = ((), (), s32[]{:S(2)}) async-start(), calls=%async_computation.3 | async-start | bytes 4194304 | tf_op jit(solution)/shard_map/psum | solution.py:27
  335.9 181.1 %all-gather.12.cloned.1.call-start = ((), (), s32[]{:S(2)}) async-start(), calls=%async_computation.6 | async-start | bytes 9437184 | tf_op jit(solution)/shard_map/all_gather | solution.py:31
  392.3 486.9 %reduce-scatter.2.cloned.1.call-start = ((), (), s32[]{:S(2)}) async-start(), calls=%async_computation.4 | async-start | bytes 9437184 | tf_op jit(solution)/shard_map/reduce_scatter | solution.py:34
  522.1 1.0 copy-start.3
  523.0 142.1 %copy-start = (f32[1024,512]{1,0:T(8,128)S(1)}, f32[1024,512]{1,0:T(8,128)}, u32[]{:S(2)}) copy-start(f32[1024,512]{1,0:T(8,128)} %all-reduce.3.cloned.1.call-done) | copy-start | bytes 6291460
  668.3 65.1 %copy-start.1 = (f32[128,1024]{1,0:T(8,128)}, f32[128,1024]{1,0:T(8,128)S(1)}, u32[]{:S(2)}) copy-start(f32[128,1024]{1,0:T(8,128)S(1)} %fusion.27) | copy-start | bytes 1572868
  671.8 4.5 copy-start.2
  676.3 0.8 copy-start.4
  733.4 272.4 %all-gather.10.cloned.1.call-start = ((), (), s32[]{:S(2)}) async-start(), calls=%async_computation.5 | async-start | bytes 9437184 | tf_op jit(solution)/shard_map/all_gather | solution.py:47
  1005.9 65.7 %slice-start = ((s8[8388608]{0:T(1024)(128)(4,1)}), s8[4194304]{0:T(1024)(128)(4,1)S(1)}, s32[]{:S(2)}) async-start(s8[8388608]{0:T(1024)(128)(4,1)} %bitcast.59), calls=%async_computation.7 | async-start | bytes 8388608
  1005.9 65.7 %slice-start.2 = ((s8[16777216]{0:T(1024)(128)(4,1)}), s8[4194304]{0:T(1024)(128)(4,1)S(1)}, s32[]{:S(2)}) async-start(s8[16777216]{0:T(1024)(128)(4,1)} %bitcast.65), calls=%async_computation.9 | async-start | bytes 8388608
  1005.9 65.7 %slice-start.3 = ((s8[16777216]{0:T(1024)(128)(4,1)}), s8[4194304]{0:T(1024)(128)(4,1)S(1)}, s32[]{:S(2)}) async-start(s8[16777216]{0:T(1024)(128)(4,1)} %bitcast.65), calls=%async_computation.10 | async-start | bytes 8388608
  1014.8 56.8 %slice-start.1 = ((s8[8388608]{0:T(1024)(128)(4,1)}), s8[4194304]{0:T(1024)(128)(4,1)S(1)}, s32[]{:S(2)}) async-start(s8[8388608]{0:T(1024)(128)(4,1)} %bitcast.59), calls=%async_computation.8 | async-start | bytes 8388608
  1014.8 56.8 %slice-start.4 = ((s8[16777216]{0:T(1024)(128)(4,1)}), s8[4194304]{0:T(1024)(128)(4,1)S(1)}, s32[]{:S(2)}) async-start(s8[16777216]{0:T(1024)(128)(4,1)} %bitcast.65), calls=%async_computation.11 | async-start | bytes 8388608
  1014.8 56.8 %slice-start.5 = ((s8[16777216]{0:T(1024)(128)(4,1)}), s8[4194304]{0:T(1024)(128)(4,1)S(1)}, s32[]{:S(2)}) async-start(s8[16777216]{0:T(1024)(128)(4,1)} %bitcast.65), calls=%async_computation.12 | async-start | bytes 8388608
Sparse Core Ops, SparseCore 0:
  9.5 37.1 all-gather.5
  48.9 227.2 all-gather.7
  336.0 49.5 all-reduce.2
  392.4 124.5 all-gather.11
  733.6 145.6 reduce-scatter.1
  881.2 124.6 all-gather.9
